TPU v7x, 128 devices: a whole 4x4x4 slice. The times are simulated.
128 devices in a mesh: dp: 32 (over x, z, y_hi), mp: 4 (over y_lo, core).
Axes of the slice: x: 4, y: 4 (y_hi: 2, y_lo: 2; y = y_hi * 2 + y_lo), z: 4, core: 2. Of those that a mesh axis runs over, the one named last changes fastest.
Arguments:
- initial_state: int32 [2048], P('dp'), may hold values from 0 to 255
- actions: int32 [2048, 16], P('dp'), may hold values from 0 to 15
- next_state: int32 [256, 16], replicated, may hold values from 0 to 255
- reward_table: float32 [256, 16], replicated, may hold values from -6 to 6
- reward_scale: float32 [2048], P('dp'), may hold values from 0.5 to 4.5
- observe_table: bfloat16 [256, 1024], replicated, may hold values from -6 to 6
- gain_attn: float32 [1024], replicated, may hold values from 0.5 to 1.5
- w_query: bfloat16 [1024, 1024], P(None, 'mp'), may hold values from -0.1875 to 0.1875
- w_key: bfloat16 [1024, 1024], P(None, 'mp'), may hold values from -0.1875 to 0.1875
- w_value: bfloat16 [1024, 1024], P(None, 'mp'), may hold values from -0.1875 to 0.1875
- w_out: bfloat16 [1024, 1024], P('mp'), may hold values from -0.1875 to 0.1875
- gain_mlp: float32 [1024], replicated, may hold values from 0.5 to 1.5
- w_up: bfloat16 [1024, 4096], P(None, 'mp'), may hold values from -0.1875 to 0.1875
- w_down: bfloat16 [4096, 1024], P('mp'), may hold values from -0.09375 to 0.09375
- gain_final: float32 [1024], replicated, may hold values from 0.5 to 1.5
- actor_head: bfloat16 [1024, 16], replicated, may hold values from -0.1875 to 0.1875
- critic_head: bfloat16 [1024], replicated, may hold values from -0.1875 to 0.1875
Outputs:
- grad_query: float32 [1024, 1024], P('dp', 'mp')
- grad_key: float32 [1024, 1024], P('dp', 'mp')
- grad_value: float32 [1024, 1024], P('dp', 'mp')
- grad_out: float32 [1024, 1024], P('mp', 'dp')
- grad_up: float32 [1024, 4096], P('dp', 'mp')
- grad_down: float32 [4096, 1024], P('mp', 'dp')
- grad_gain_attn: float32 [1024], P(('dp', 'mp'))
- grad_gain_mlp: float32 [1024], P('dp')
- grad_gain_final: float32 [1024], P('dp')
- grad_actor: float32 [1024, 16], P('dp')
- grad_critic: float32 [1024], P('dp')
All inputs are finite; a program needn't handle non-finite values.
Results may differ from a plain program's by a relative error of at most 0.015.
Values sent between devices are 32-bit elements; how exact they have to be, the bound alone decides.
A program may use at most 128 MiB of HBM per device.

v0:
```python
import math
import jax
import jax.numpy as jnp
from jax import lax
from jax.sharding import PartitionSpec as P

HEAD_DIM = 128
STEPS = 16
EPS = 1e-05
GAMMA = 0.9
VALUE_COEF = 0.5
ENTROPY_COEF = 0.1


def from_everyone(value, axis):
    copies = jnp.broadcast_to(value, (lax.axis_size(axis), *value.shape))
    return lax.all_to_all(copies, axis, split_axis=0, concat_axis=0, tiled=True)


def taken_together(value, axis):
    everything = from_everyone(value, axis)
    return jnp.sum(everything, axis=0)


def together(arrays, axis):
    ends = [0]
    for a in arrays:
        ends.append(ends[-1] + a.size)
    running = taken_together(jnp.concatenate([a.ravel() for a in arrays]), axis)
    return tuple((running[b:e].reshape(a.shape) for a, b, e in zip(arrays, ends, ends[1:])))


def side_by_side(arrays, axis, dim, along):
    both = jnp.concatenate(arrays, axis=along)
    out, at, done = (lax.psum_scatter(both, axis, scatter_dimension=dim, tiled=True), 0, [])
    for a in arrays:
        done.append(lax.slice_in_dim(out, at, at + a.shape[along], axis=along))
        at += a.shape[along]
    return tuple(done)


def sent_together(arrays, axis, dim, along):
    widths = [math.prod(a.shape[along:]) for a in arrays]
    both = jnp.concatenate(
        [a.reshape(*a.shape[:along], w) for a, w in zip(arrays, widths)], axis=along
    )
    out = lax.psum_scatter(both, axis, scatter_dimension=dim, tiled=True)
    blocks = jnp.split(out, [sum(widths[:k]) for k in range(1, len(widths))], axis=along)
    return tuple((b.reshape(*out.shape[:along], *a.shape[along:]) for a, b in zip(arrays, blocks)))


def roll_states(initial_state, actions, next_state):
    flat_table = next_state.reshape(-1)
    table_width = next_state.shape[1]
    cell_ids = jnp.arange(flat_table.shape[0], dtype=jnp.int32)

    def advance(current, action):
        flat_index = current * table_width + action
        chosen = jnp.sum(
            jnp.where(flat_index[:, None] == cell_ids[None, :], flat_table[None, :], 0), axis=1
        )
        return (chosen, current)

    unused, visited = lax.scan(advance, initial_state, jnp.transpose(actions))
    return jnp.transpose(visited)


def state_tables(states, actions, reward_table, reward_scale, observe_table):
    state_count = reward_table.shape[0]
    state_match = states.reshape(-1)[:, None] == jnp.arange(state_count, dtype=jnp.int32)[None, :]
    reward_rows = jnp.dot(
        state_match.astype(jnp.float32),
        reward_table,
        precision=lax.Precision.HIGHEST,
        preferred_element_type=jnp.float32,
    )
    chosen = (
        actions.reshape(-1)[:, None] == jnp.arange(reward_table.shape[1], dtype=jnp.int32)[None, :]
    )
    rewards = (
        jnp.sum(jnp.where(chosen, reward_rows, 0.0), axis=1).reshape(states.shape)
        * reward_scale[:, None]
    )
    embedded = jnp.dot(
        state_match.astype(jnp.bfloat16), observe_table, preferred_element_type=jnp.float32
    )
    return (rewards, embedded)


def normalize(inputs, gain):
    inverse_rms = lax.rsqrt(jnp.mean(inputs * inputs, axis=-1, keepdims=True) + EPS)
    return (inputs * inverse_rms * gain, inverse_rms)


def norm_back(inputs, inverse_rms, gain, upstream):
    weighted = upstream * gain
    return inverse_rms * weighted - inputs * inverse_rms**3 * jnp.mean(
        inputs * weighted, axis=-1, keepdims=True
    )


def discount(rewards, critic_grid):

    def backward_step(running, reward):
        running = reward + GAMMA * running
        return (running, running)

    unused, totals = lax.scan(
        backward_step, critic_grid[:, -1], jnp.transpose(rewards), reverse=True
    )
    return jnp.transpose(totals)


def policy_terms(logits, critic_out, returns, normed, actions, factor):
    logp = logits - jnp.log(jnp.sum(jnp.exp(logits), axis=1, keepdims=True))
    chance = jnp.exp(logp)
    entropy = -jnp.sum(chance * logp, axis=1, keepdims=True)
    picked = (
        actions.reshape(-1)[:, None] == jnp.arange(logits.shape[1], dtype=jnp.int32)[None, :]
    ).astype(jnp.float32)
    d_logits = factor * (
        -normed.reshape(-1)[:, None] * (picked - chance) + ENTROPY_COEF * chance * (logp + entropy)
    )
    d_value = factor * VALUE_COEF * (critic_out - returns.reshape(-1))
    return (d_logits.astype(jnp.bfloat16), d_value.astype(jnp.bfloat16))


def product(left, right):
    return jnp.dot(left, right, preferred_element_type=jnp.float32)


def across(left, right):
    return jnp.dot(left.T, right, preferred_element_type=jnp.float32)


def heads_view(rows_array):
    return rows_array.reshape(rows_array.shape[0] // STEPS, STEPS, -1, HEAD_DIM)


def attend(queries, key_rows, value_rows):
    q_heads, k_heads, v_heads = (heads_view(queries), heads_view(key_rows), heads_view(value_rows))
    scores = jnp.einsum(
        "eqhd,ekhd->ehqk", q_heads, k_heads, preferred_element_type=jnp.float32
    ) / math.sqrt(HEAD_DIM)
    causal = jnp.arange(STEPS)[:, None] >= jnp.arange(STEPS)[None, :]
    weights = jnp.where(causal, jnp.exp(scores), 0.0)
    attn_probs = weights / jnp.sum(weights, axis=-1, keepdims=True)
    probs_low = attn_probs.astype(jnp.bfloat16)
    mixed_rows = jnp.einsum(
        "ehqk,ekhd->eqhd", probs_low, v_heads, preferred_element_type=jnp.float32
    )
    return (mixed_rows.astype(jnp.bfloat16).reshape(queries.shape), attn_probs, probs_low)


def attend_back(queries, key_rows, value_rows, attn_probs, probs_low, d_mixed):
    q_heads, k_heads, v_heads = (heads_view(queries), heads_view(key_rows), heads_view(value_rows))
    d_heads = heads_view(d_mixed)
    d_probs = jnp.einsum("eqhd,ekhd->ehqk", d_heads, v_heads, preferred_element_type=jnp.float32)
    d_values = jnp.einsum(
        "ehqk,eqhd->ekhd", probs_low, d_heads, preferred_element_type=jnp.float32
    ).astype(jnp.bfloat16)
    d_scores = (
        attn_probs
        * (d_probs - jnp.sum(attn_probs * d_probs, axis=-1, keepdims=True))
        / math.sqrt(HEAD_DIM)
    ).astype(jnp.bfloat16)
    d_queries = jnp.einsum(
        "ehqk,ekhd->eqhd", d_scores, k_heads, preferred_element_type=jnp.float32
    ).astype(jnp.bfloat16)
    d_keys = jnp.einsum(
        "ehqk,eqhd->ekhd", d_scores, q_heads, preferred_element_type=jnp.float32
    ).astype(jnp.bfloat16)
    return (
        d_queries.reshape(queries.shape),
        d_keys.reshape(queries.shape),
        d_values.reshape(queries.shape),
    )


def per_device(
    initial_state,
    actions,
    next_state,
    reward_table,
    reward_scale,
    observe_table,
    gain_attn,
    w_query,
    w_key,
    w_value,
    w_out,
    gain_mlp,
    w_up,
    w_down,
    gain_final,
    actor_head,
    critic_head,
):
    states = roll_states(initial_state, actions, next_state)
    rewards, x_zero = state_tables(states, actions, reward_table, reward_scale, observe_table)
    h_one, n_one = normalize(x_zero, gain_attn)
    h_one = h_one.astype(jnp.bfloat16)
    queries = product(h_one, w_query).astype(jnp.bfloat16)
    key_rows = product(h_one, w_key).astype(jnp.bfloat16)
    value_rows = product(h_one, w_value).astype(jnp.bfloat16)
    mixed_rows, attn_probs, probs_low = attend(queries, key_rows, value_rows)
    x_one = x_zero + lax.psum(product(mixed_rows, w_out), "mp")
    h_two, n_two = normalize(x_one, gain_mlp)
    h_two = h_two.astype(jnp.bfloat16)
    up_rows = product(h_two, w_up)
    hidden = jax.nn.silu(up_rows).astype(jnp.bfloat16)
    x_two = x_one + lax.psum(product(hidden, w_down), "mp")
    final_rows, n_fin = normalize(x_two, gain_final)
    final_rows = final_rows.astype(jnp.bfloat16)
    logits = product(final_rows, actor_head)
    critic_out = jnp.dot(final_rows, critic_head, preferred_element_type=jnp.float32)
    env_count = actions.shape[0]
    critic_grid = critic_out.reshape(env_count, STEPS)
    returns = discount(rewards, critic_grid)
    advantage = returns - critic_grid
    token_total = advantage.size * lax.axis_size("dp")
    adv_sum, adv_square = together((jnp.sum(advantage), jnp.sum(advantage * advantage)), "dp")
    adv_mean = adv_sum / token_total
    spread = adv_square / token_total - adv_mean * adv_mean
    normed = (advantage - adv_mean) * lax.rsqrt(spread + EPS)
    d_logits, d_value = policy_terms(
        logits, critic_out, returns, normed, actions, 1.0 / math.sqrt(token_total)
    )
    grad_actor = across(final_rows, d_logits)
    grad_critic = jnp.dot(d_value, final_rows, preferred_element_type=jnp.float32)
    d_final = (
        product(d_logits, actor_head.T)
        + d_value[:, None].astype(jnp.float32) * critic_head.astype(jnp.float32)[None, :]
    )
    grad_final = jnp.sum(d_final * x_two * n_fin, axis=0)
    dx_two = norm_back(x_two, n_fin, gain_final, d_final)
    dx_two_low = dx_two.astype(jnp.bfloat16)
    grad_down = across(hidden, dx_two_low)
    d_hidden = product(dx_two_low, w_down.T).astype(jnp.bfloat16)
    sigmoid_up = jax.nn.sigmoid(up_rows)
    d_up = (
        d_hidden.astype(jnp.float32) * sigmoid_up * (1.0 + up_rows * (1.0 - sigmoid_up))
    ).astype(jnp.bfloat16)
    grad_up = across(h_two, d_up)
    d_h_two = lax.psum(product(d_up, w_up.T), "mp")
    grad_mlp = jnp.sum(d_h_two * x_one * n_two, axis=0)
    dx_one = dx_two + norm_back(x_one, n_two, gain_mlp, d_h_two)
    dx_one_low = dx_one.astype(jnp.bfloat16)
    grad_out = across(mixed_rows, dx_one_low)
    d_mixed = product(dx_one_low, w_out.T).astype(jnp.bfloat16)
    d_queries, d_keys, d_values = attend_back(
        queries, key_rows, value_rows, attn_probs, probs_low, d_mixed
    )
    grad_query = across(h_one, d_queries)
    grad_key = across(h_one, d_keys)
    grad_value = across(h_one, d_values)
    (
        query_part,
        key_part,
        value_part,
        out_total,
        up_part,
        down_part,
        mlp_total,
        final_total,
        actor_total,
        critic_total,
    ) = (
        *side_by_side((grad_query, grad_key, grad_value), "dp", 0, 1),
        lax.psum_scatter(grad_out, "dp", scatter_dimension=1, tiled=True),
        lax.psum_scatter(grad_up, "dp", scatter_dimension=0, tiled=True),
        lax.psum_scatter(grad_down, "dp", scatter_dimension=1, tiled=True),
        lax.psum_scatter(grad_mlp, "dp", scatter_dimension=0, tiled=True),
        *sent_together((grad_final, grad_actor, grad_critic), "dp", 0, 1),
    )
    d_h_one = (
        product(d_queries, w_query.T) + product(d_keys, w_key.T) + product(d_values, w_value.T)
    )
    attn_term = jnp.sum(d_h_one * x_zero * n_one, axis=0)
    attn_total = lax.psum_scatter(attn_term, ("dp", "mp"), scatter_dimension=0, tiled=True)
    return (
        query_part,
        key_part,
        value_part,
        out_total,
        up_part,
        down_part,
        attn_total,
        mlp_total,
        final_total,
        actor_total,
        critic_total,
    )


def solution(mesh):
    return jax.shard_map(
        per_device,
        mesh=mesh,
        in_specs=(
            P("dp"),
            P("dp", None),
            P(),
            P(),
            P("dp"),
            P(),
            P(),
            P(None, "mp"),
            P(None, "mp"),
            P(None, "mp"),
            P("mp", None),
            P(),
            P(None, "mp"),
            P("mp", None),
            P(),
            P(),
            P(),
        ),
        out_specs=(
            P("dp", "mp"),
            P("dp", "mp"),
            P("dp", "mp"),
            P("mp", "dp"),
            P("dp", "mp"),
            P("mp", "dp"),
            P(("dp", "mp")),
            P("dp"),
            P("dp"),
            P("dp", None),
            P("dp"),
        ),
        check_vma=False,
    )
```

profile of v0, /device:TPU:0, one launch (start us, length us, event | category | flops | bytes accessed | tf_op | source)
XLA Modules:
  0.0 1380.3 jit_solution(4627892525124628884)
XLA Ops:
  9.5 16.5 %while.31 = (s32[]{:T(128)}, s32[64]{0:T(128)S(1)}, s32[16,64]{1,0:T(8,128)S(1)}, s32[16,64]{1,0:T(8,128)}, s32[256,16]{1,0:T(8,128)}, /*index=5*/s32[4096]{0:T(1024)S(1)}, s32[]{:T(128)}, s32[]{:T(128)}) while((s32[]{:T(128)}, s32[64]{0:T(128)S(1)}, s32[16,64]{1,0:T(8,128)S(1)}, s32[16,64]{1,0:T(8,128)}, ...), condition=%wide.wide.region_2.3_spmd.clone, body=%wide.wide.region_0.2_spmd.clone.sunk | while | flops 786498 | bytes 18277 | solution.py:64
  39.5 2.7 fusion.7
  42.2 2.8 fusion.9
  47.2 2.7 fusion.36
  50.4 93.4 %all-reduce.6.cloned.1.call-done = f32[1024,1024]{0,1:T(8,128)} async-done(((f32[1024,1024]{0,1:T(8,128)}), f32[1024,1024]{0,1:T(8,128)}) %all-reduce.6.cloned.1.call-update) | async-done | bytes 4194320 | tf_op jit(solution)/shard_map/psum | solution.py:207
  143.8 4.6 multiply_reduce_fusion.6
  153.0 4.4 fusion.82
  159.1 90.6 %all-reduce.8.cloned.1.call-done = f32[1024,1024]{0,1:T(8,128)} async-done(((f32[1024,1024]{0,1:T(8,128)}), f32[1024,1024]{0,1:T(8,128)}) %all-reduce.8.cloned.1.call-update) | async-done | bytes 4194320 | tf_op jit(solution)/shard_map/psum | solution.py:212
  249.7 4.5 multiply_reduce_fusion.5
  261.1 9.4 all-to-all-start
  273.1 7.0 all-to-all-done
  283.5 3.7 multiply_reduce_fusion
  289.5 3.5 multiply_convert_fusion
  294.3 4.3 fusion.88
  298.7 2.9 fusion.39
  304.2 80.9 %all-reduce.10.cloned.1.call-done = f32[1024,1024]{0,1:T(8,128)} async-done(((f32[1024,1024]{0,1:T(8,128)}), f32[1024,1024]{0,1:T(8,128)}) %all-reduce.10.cloned.1.call-update) | async-done | bytes 4194320 | tf_op jit(solution)/shard_map/psum | solution.py:245
  385.1 4.6 multiply_reduce_fusion.1
  391.0 3.2 add_convert_fusion
  398.4 2.8 fusion.12
  402.6 3.8 fusion.10
  406.4 3.5 fusion.11
  419.5 3.6 copy.203
  423.2 3.3 fusion.34
  426.5 7.9 fusion.14
  436.0 6.5 fusion.80
  444.4 130.1 %reduce-scatter.18.cloned.1.call-done = f32[32,18]{1,0:T(8,128)} async-done(((f32[1024,18]{1,0:T(8,128)}), f32[32,18]{1,0:T(8,128)}) %reduce-scatter.18.cloned.1.call-update) | async-done | bytes 2320
  578.0 89.5 %all-reduce.1 = f32[1024]{0:T(1024)S(1)} all-reduce(f32[1024]{0:T(1024)S(1)} %get-tuple-element.254), channel_id=7, replica_groups=mesh['dp'=32,'mp'=4] {'dp'}, use_global_device_ids=true, to_apply=%region_28.29.clone | all-reduce | flops 1024 | bytes 8192
  672.8 63.2 %all-reduce = f32[1024]{0:T(1024)S(1)} all-reduce(f32[1024]{0:T(1024)S(1)} %multiply_reduce_fusion.2), channel_id=6, replica_groups=mesh['dp'=32,'mp'=4] {'dp','mp'}, use_global_device_ids=true, to_apply=%region_26.27.clone | all-reduce | flops 1024 | bytes 8192
  736.6 65.9 %reduce-scatter.16.cloned.1.call-done = f32[32,768]{1,0:T(8,128)} async-done(((f32[1024,768]{1,0:T(8,128)}), f32[32,768]{1,0:T(8,128)}) %reduce-scatter.16.cloned.1.call-update) | async-done | bytes 98320
  804.0 185.6 %reduce-scatter.10.cloned.1.call-done = f32[256,32]{0,1:T(8,128)} async-done(((f32[256,1024]{0,1:T(8,128)}), f32[256,32]{0,1:T(8,128)}) %reduce-scatter.10.cloned.1.call-update) | async-done | bytes 32784 | tf_op jit(solution)/shard_map/reduce_scatter | solution.py:270
  989.5 191.6 %reduce-scatter.14.cloned.1.call-done = f32[1024,32]{0,1:T(8,128)} async-done(((f32[1024,1024]{0,1:T(8,128)}), f32[1024,32]{0,1:T(8,128)}) %reduce-scatter.14.cloned.1.call-update) | async-done | bytes 131088 | tf_op jit(solution)/shard_map/reduce_scatter | solution.py:272
  1181.1 192.2 %reduce-scatter.12.cloned.1.call-done = f32[32,1024]{1,0:T(8,128)} async-done(((f32[1024,1024]{1,0:T(8,128)}), f32[32,1024]{1,0:T(8,128)}) %reduce-scatter.12.cloned.1.call-update) | async-done | bytes 131088 | tf_op jit(solution)/shard_map/reduce_scatter | solution.py:271
  (254 shorter events, 87.9 us)
Async XLA Ops:
  7.2 145.8 %copy-start = (bf16[1024,1024]{1,0:T(8,128)(2,1)S(1)}, bf16[1024,1024]{1,0:T(8,128)(2,1)}, u32[]{:S(2)}) copy-start(bf16[1024,1024]{1,0:T(8,128)(2,1)} %param.34) | copy-start | bytes 6291460
  7.2 136.6 %all-reduce.6.cloned.1.call-start = ((), (), s32[]{:S(2)}) async-start(), calls=%async_computation.6 | async-start | bytes 8388608 | tf_op jit(solution)/shard_map/psum | solution.py:207
  8.9 21.2 %copy-start.30 = (f32[1024]{0:T(1024)S(1)}, f32[1024]{0:T(1024)}, u32[]{:S(2)}) copy-start(f32[1024]{0:T(1024)} %param.27) | copy-start | bytes 12292
  28.2 3.7 copy-start.20
  39.5 7.7 copy-start.19
  50.0 98.4 %copy-start.27 = (f32[1024]{0:T(1024)S(1)}, f32[1024]{0:T(1024)}, u32[]{:S(2)}) copy-start(f32[1024]{0:T(1024)} %param.32) | copy-start | bytes 12292
  50.0 199.7 %all-reduce.8.cloned.1.call-start = ((), (), s32[]{:S(2)}) async-start(), calls=%async_computation.7 | async-start | bytes 8388608 | tf_op jit(solution)/shard_map/psum | solution.py:212
  143.8 4.6 copy-start.32
  148.4 2.6 copy-start.4
  159.1 95.1 %copy-start.26 = (f32[1024]{0:T(1024)S(1)}, f32[1024]{0:T(1024)}, u32[]{:S(2)}) copy-start(f32[1024]{0:T(1024)} %param.35) | copy-start | bytes 12292
  254.2 2.7 copy-start.8
  254.2 16.8 %copy-start.25 = (bf16[1024,16]{0,1:T(8,128)(2,1)S(1)}, bf16[1024,16]{0,1:T(8,128)(2,1)}, u32[]{:S(2)}) copy-start(bf16[1024,16]{0,1:T(8,128)(2,1)} %param.36) | copy-start | bytes 98308
  261.1 19.1 %all-to-all-start = ((f32[32,1,2]{2,1,0:T(1,128)}), f32[32,1,2]{2,1,0:T(1,128)S(1)}, u32[]{:S(2)}, u32[]{:S(2)}) async-start(f32[32,1,2]{2,1,0:T(1,128)} %broadcast_in_dim.78), calls=%async_computation | async-start | bytes 32768 | tf_op jit(solution)/shard_map/all_to_all | solution.py:17
  270.5 114.6 %all-reduce.10.cloned.1.call-start = ((), (), s32[]{:S(2)}) async-start(), calls=%async_computation.8 | async-start | bytes 8388608 | tf_op jit(solution)/shard_map/psum | solution.py:245
  283.5 3.7 copy-start.9
  289.5 3.5 copy-start.12
  289.5 4.8 copy-start.33
  298.6 3.0 copy-start.7
  298.7 275.9 %reduce-scatter.18.cloned.1.call-start = ((), (), s32[]{:S(2)}) async-start(), calls=%async_computation.13 | async-start | bytes 540672
  304.0 498.6 %reduce-scatter.16.cloned.1.call-start = ((), (), s32[]{:S(2)}) async-start(), calls=%async_computation.12 | async-start | bytes 3244032
  385.1 4.7 copy-start.5
  385.1 5.9 copy-start.13
  398.4 8.0 copy-start.23
  402.6 12.5 copy-start.11
  419.5 3.7 copy-start.17
  423.1 566.4 %reduce-scatter.10.cloned.1.call-start = ((), (), s32[]{:S(2)}) async-start(), calls=%async_computation.9 | async-start | bytes 1081344 | tf_op jit(solution)/shard_map/reduce_scatter | solution.py:270
  426.5 754.6 %reduce-scatter.14.cloned.1.call-start = ((), (), s32[]{:S(2)}) async-start(), calls=%async_computation.11 | async-start | bytes 4325376 | tf_op jit(solution)/shard_map/reduce_scatter | solution.py:272
  434.4 938.8 %reduce-scatter.12.cloned.1.call-start = ((), (), s32[]{:S(2)}) async-start(), calls=%async_computation.10 | async-start | bytes 4325376 | tf_op jit(solution)/shard_map/reduce_scatter | solution.py:271
  442.5 225.6 %copy-start.24 = (bf16[1024,256]{1,0:T(8,128)(2,1)S(1)}, bf16[1024,256]{1,0:T(8,128)(2,1)}, u32[]{:S(2)}) copy-start(bf16[1024,256]{1,0:T(8,128)(2,1)} %param.29) | copy-start | bytes 1572868
  668.9 2.5 copy-start.15
  668.9 2.6 copy-start.21
  668.9 704.4 %copy-start.1 = (bf16[1024,1024]{1,0:T(8,128)(2,1)S(1)}, bf16[1024,1024]{1,0:T(8,128)(2,1)}, u32[]{:S(2)}) copy-start(bf16[1024,1024]{1,0:T(8,128)(2,1)} %param.34) | copy-start | bytes 6291460
  (17 other events, 22.6 us)
Sparse Core Ops, SparseCore 0:
  50.1 93.6 all-reduce.5
  157.5 92.1 all-reduce.7
  298.8 86.3 all-reduce.9
  387.3 187.1 reduce-scatter.17
  579.4 223.0 reduce-scatter.15
  805.3 184.1 reduce-scatter.9
  992.5 188.5 reduce-scatter.13
  1184.0 189.1 reduce-scatter.11
where the time goes:
time: 1390 us; the launch traced here: 1380 us
  waiting for transfers between devices  1040 us (75%)
  blocking collectives  153 us (11%)
  matrix products  75.5 us (5%)
  other arithmetic  42.6 us (3%)
  local copies, waits for them, and re-layouts  42.4 us (3%)
  between operations  18.2 us (1%)
    unnamed x10, waiting for transfers between devices  196 us
    reduce_scatter x1, waiting for transfers between devices, per_device(): lax.psum_scatter(grad_up, 'dp', scatter_dimension=0, tiled=True)  192 us
    reduce_scatter x1, waiting for transfers between devices, per_device(): lax.psum_scatter(grad_down, 'dp', scatter_dimension=1, tiled=True)  192 us
    reduce_scatter x1, waiting for transfers between devices, per_device(): lax.psum_scatter(grad_out, 'dp', scatter_dimension=1, tiled=True)  186 us
    unnamed x2, blocking collectives  153 us
    psum x1, waiting for transfers between devices, per_device(): x_one = x_zero + lax.psum(product(mixed_rows, w_out), 'mp')  93.4 us
    psum x1, waiting for transfers between devices, per_device(): x_two = x_one + lax.psum(product(hidden, w_down), 'mp')  90.6 us
    psum x1, waiting for transfers between devices, per_device(): d_h_two = lax.psum(product(d_up, w_up.T), 'mp')  80.9 us
  transfers between devices with their start and end apart: 9, of which 9 were waited for; matrix products, arithmetic and copies ran while one was open for 5% of the time, Pallas kernels for 0%

commit v1 on v0

--- a/solution.py
+++ b/solution.py
@@ -242,7 +242,7 @@
         d_hidden.astype(jnp.float32) * sigmoid_up * (1.0 + up_rows * (1.0 - sigmoid_up))
     ).astype(jnp.bfloat16)
     grad_up = across(h_two, d_up)
-    d_h_two = lax.psum(product(d_up, w_up.T), "mp")
+    d_h_two = jnp.sum(lax.all_gather(product(d_up, w_up.T), "mp"), axis=0)
     grad_mlp = jnp.sum(d_h_two * x_one * n_two, axis=0)
     dx_one = dx_two + norm_back(x_one, n_two, gain_mlp, d_h_two)
     dx_one_low = dx_one.astype(jnp.bfloat16)

time: 1390 us -> 1450 us (1.043)
  waiting for transfers between devices: 1040 us -> 1080 us
    all_gather x0 -> x1, waiting for transfers between devices: none -> 139 us  [per_device(): d_h_two = jnp.sum(lax.all_gather(product(d_up, w_up.T), 'mp'), axis=0)]
    psum x1 -> x0, waiting for transfers between devices: 80.9 us -> none  [per_device(): d_h_two = lax.psum(product(d_up, w_up.T), 'mp')]
    unnamed x10, waiting for transfers between devices: 196 us -> 182 us
  transfers between devices with their start and end apart: 9 -> 9, of which waited for: 9 -> 9; matrix products, arithmetic and copies ran while one was open for 5% -> 6% of each run, Pallas kernels for 0% -> 0%
where the time goes in v1:
time: 1450 us; the launch traced here: 1440 us
  waiting for transfers between devices  1080 us (74%)
  blocking collectives  153 us (11%)
  matrix products  75.9 us (5%)
  other arithmetic  53 us (4%)
  local copies, waits for them, and re-layouts  48.2 us (3%)
  between operations  18.2 us (1%)
    reduce_scatter x1, waiting for transfers between devices, per_device(): lax.psum_scatter(grad_up, 'dp', scatter_dimension=0, tiled=True)  193 us
    reduce_scatter x1, waiting for transfers between devices, per_device(): lax.psum_scatter(grad_down, 'dp', scatter_dimension=1, tiled=True)  193 us
    reduce_scatter x1, waiting for transfers between devices, per_device(): lax.psum_scatter(grad_out, 'dp', scatter_dimension=1, tiled=True)  185 us
    unnamed x10, waiting for transfers between devices  182 us
    unnamed x2, blocking collectives  153 us
    all_gather x1, waiting for transfers between devices, per_device(): d_h_two = jnp.sum(lax.all_gather(product(d_up, w_up.T), 'mp'), axis=0)  139 us
    psum x1, waiting for transfers between devices, per_device(): x_one = x_zero + lax.psum(product(mixed_rows, w_out), 'mp')  93.4 us
    psum x1, waiting for transfers between devices, per_device(): x_two = x_one + lax.psum(product(hidden, w_down), 'mp')  90.6 us
  transfers between devices with their start and end apart: 9, of which 9 were waited for; matrix products, arithmetic and copies ran while one was open for 6% of the time, Pallas kernels for 0%

profile of v1, /device:TPU:0, one launch (start us, length us, event | category | flops | bytes accessed | tf_op | source)
XLA Modules:
  0.0 1442.0 jit_solution(16654885393241418960)
XLA Ops:
  9.5 16.5 %while.31 = (s32[]{:T(128)}, s32[64]{0:T(128)S(1)}, s32[16,64]{1,0:T(8,128)S(1)}, s32[16,64]{1,0:T(8,128)}, s32[256,16]{1,0:T(8,128)}, /*index=5*/s32[4096]{0:T(1024)S(1)}, s32[]{:T(128)}, s32[]{:T(128)}) while((s32[]{:T(128)}, s32[64]{0:T(128)S(1)}, s32[16,64]{1,0:T(8,128)S(1)}, s32[16,64]{1,0:T(8,128)}, ...), condition=%wide.wide.region_2.3_spmd.clone, body=%wide.wide.region_0.2_spmd.clone.sunk | while | flops 786498 | bytes 18277 | solution.py:64
  42.1 2.9 fusion.9
  50.4 93.4 %all-reduce.5.cloned.1.call-done = f32[1024,1024]{0,1:T(8,128)} async-done(((f32[1024,1024]{0,1:T(8,128)}), f32[1024,1024]{0,1:T(8,128)}) %all-reduce.5.cloned.1.call-update) | async-done | bytes 4194320 | tf_op jit(solution)/shard_map/psum | solution.py:207
  143.8 4.6 multiply_reduce_fusion.6
  153.0 4.4 fusion.82
  159.2 90.6 %all-reduce.7.cloned.1.call-done = f32[1024,1024]{0,1:T(8,128)} async-done(((f32[1024,1024]{0,1:T(8,128)}), f32[1024,1024]{0,1:T(8,128)}) %all-reduce.7.cloned.1.call-update) | async-done | bytes 4194320 | tf_op jit(solution)/shard_map/psum | solution.py:212
  249.8 4.5 multiply_reduce_fusion.5
  261.1 9.4 all-to-all-start
  273.2 7.0 all-to-all-done
  283.6 3.7 multiply_reduce_fusion
  289.5 3.5 multiply_convert_fusion
  294.3 4.4 fusion.88
  298.8 2.9 fusion.39
  304.2 139.0 %all-gather.3.cloned.1.call-done = f32[4096,1024]{1,0:T(8,128)} async-done(((f32[1024,1024]{1,0:T(8,128)}), f32[4096,1024]{1,0:T(8,128)}) %all-gather.3.cloned.1.call-update) | async-done | bytes 16777232 | tf_op jit(solution)/shard_map/all_gather | solution.py:245
  443.2 10.4 reduce_sum.173
  453.6 5.4 copy.177
  459.0 4.6 multiply_reduce_fusion.1
  464.9 3.2 add_convert_fusion
  472.2 2.9 fusion.12
  476.6 3.8 fusion.10
  480.4 3.5 fusion.11
  493.5 3.6 copy.202
  497.5 7.8 fusion.14
  506.9 6.5 fusion.80
  514.5 3.3 fusion.34
  519.0 115.4 %reduce-scatter.18.cloned.1.call-done = f32[32,18]{1,0:T(8,128)} async-done(((f32[1024,18]{1,0:T(8,128)}), f32[32,18]{1,0:T(8,128)}) %reduce-scatter.18.cloned.1.call-update) | async-done | bytes 2320
  637.9 89.4 %all-reduce.1 = f32[1024]{0:T(1024)S(1)} all-reduce(f32[1024]{0:T(1024)S(1)} %get-tuple-element.254), channel_id=8, replica_groups=mesh['dp'=32,'mp'=4] {'dp'}, use_global_device_ids=true, to_apply=%region_28.29.clone | all-reduce | flops 1024 | bytes 8192
  732.6 63.3 %all-reduce = f32[1024]{0:T(1024)S(1)} all-reduce(f32[1024]{0:T(1024)S(1)} %multiply_reduce_fusion.2), channel_id=7, replica_groups=mesh['dp'=32,'mp'=4] {'dp','mp'}, use_global_device_ids=true, to_apply=%region_26.27.clone | all-reduce | flops 1024 | bytes 8192
  796.5 66.1 %reduce-scatter.16.cloned.1.call-done = f32[32,768]{1,0:T(8,128)} async-done(((f32[1024,768]{1,0:T(8,128)}), f32[32,768]{1,0:T(8,128)}) %reduce-scatter.16.cloned.1.call-update) | async-done | bytes 98320
  864.1 192.8 %reduce-scatter.14.cloned.1.call-done = f32[1024,32]{0,1:T(8,128)} async-done(((f32[1024,1024]{0,1:T(8,128)}), f32[1024,32]{0,1:T(8,128)}) %reduce-scatter.14.cloned.1.call-update) | async-done | bytes 131088 | tf_op jit(solution)/shard_map/reduce_scatter | solution.py:272
  1056.8 193.2 %reduce-scatter.12.cloned.1.call-done = f32[32,1024]{1,0:T(8,128)} async-done(((f32[1024,1024]{1,0:T(8,128)}), f32[32,1024]{1,0:T(8,128)}) %reduce-scatter.12.cloned.1.call-update) | async-done | bytes 131088 | tf_op jit(solution)/shard_map/reduce_scatter | solution.py:271
  1250.0 184.9 %reduce-scatter.10.cloned.1.call-done = f32[256,32]{0,1:T(8,128)} async-done(((f32[256,1024]{0,1:T(8,128)}), f32[256,32]{0,1:T(8,128)}) %reduce-scatter.10.cloned.1.call-update) | async-done | bytes 32784 | tf_op jit(solution)/shard_map/reduce_scatter | solution.py:270
  (256 shorter events, 93.8 us)
Async XLA Ops:
  7.2 145.9 %copy-start = (bf16[1024,1024]{1,0:T(8,128)(2,1)S(1)}, bf16[1024,1024]{1,0:T(8,128)(2,1)}, u32[]{:S(2)}) copy-start(bf16[1024,1024]{1,0:T(8,128)(2,1)} %param.34) | copy-start | bytes 6291460
  7.2 136.6 %all-reduce.5.cloned.1.call-start = ((), (), s32[]{:S(2)}) async-start(), calls=%async_computation.6 | async-start | bytes 8388608 | tf_op jit(solution)/shard_map/psum | solution.py:207
  8.9 21.2 %copy-start.30 = (f32[1024]{0:T(1024)S(1)}, f32[1024]{0:T(1024)}, u32[]{:S(2)}) copy-start(f32[1024]{0:T(1024)} %param.27) | copy-start | bytes 12292
  28.2 3.6 copy-start.20
  39.4 7.9 copy-start.19
  50.0 98.4 %copy-start.27 = (f32[1024]{0:T(1024)S(1)}, f32[1024]{0:T(1024)}, u32[]{:S(2)}) copy-start(f32[1024]{0:T(1024)} %param.32) | copy-start | bytes 12292
  50.0 199.8 %all-reduce.7.cloned.1.call-start = ((), (), s32[]{:S(2)}) async-start(), calls=%async_computation.7 | async-start | bytes 8388608 | tf_op jit(solution)/shard_map/psum | solution.py:212
  143.8 4.6 copy-start.32
  148.4 2.6 copy-start.4
  159.2 95.1 %copy-start.26 = (f32[1024]{0:T(1024)S(1)}, f32[1024]{0:T(1024)}, u32[]{:S(2)}) copy-start(f32[1024]{0:T(1024)} %param.35) | copy-start | bytes 12292
  254.3 2.6 copy-start.8
  254.3 16.8 %copy-start.25 = (bf16[1024,16]{0,1:T(8,128)(2,1)S(1)}, bf16[1024,16]{0,1:T(8,128)(2,1)}, u32[]{:S(2)}) copy-start(bf16[1024,16]{0,1:T(8,128)(2,1)} %param.36) | copy-start | bytes 98308
  261.1 19.1 %all-to-all-start = ((f32[32,1,2]{2,1,0:T(1,128)}), f32[32,1,2]{2,1,0:T(1,128)S(1)}, u32[]{:S(2)}, u32[]{:S(2)}) async-start(f32[32,1,2]{2,1,0:T(1,128)} %broadcast_in_dim.78), calls=%async_computation | async-start | bytes 32768 | tf_op jit(solution)/shard_map/all_to_all | solution.py:17
  270.5 172.7 %all-gather.3.cloned.1.call-start = ((), (), s32[]{:S(2)}) async-start(), calls=%async_computation.11 | async-start | bytes 20971520 | tf_op jit(solution)/shard_map/all_gather | solution.py:245
  283.6 3.7 copy-start.9
  289.4 3.5 copy-start.13
  289.5 4.8 copy-start.33
  298.7 2.9 copy-start.7
  298.7 335.7 %reduce-scatter.18.cloned.1.call-start = ((), (), s32[]{:S(2)}) async-start(), calls=%async_computation.13 | async-start | bytes 540672
  304.0 558.6 %reduce-scatter.16.cloned.1.call-start = ((), (), s32[]{:S(2)}) async-start(), calls=%async_computation.12 | async-start | bytes 3244032
  459.0 4.7 copy-start.5
  459.0 5.9 copy-start.10
  472.2 8.2 copy-start.23
  476.6 12.5 copy-start.12
  497.2 559.6 %reduce-scatter.14.cloned.1.call-start = ((), (), s32[]{:S(2)}) async-start(), calls=%async_computation.10 | async-start | bytes 4325376 | tf_op jit(solution)/shard_map/reduce_scatter | solution.py:272
  505.3 744.7 %reduce-scatter.12.cloned.1.call-start = ((), (), s32[]{:S(2)}) async-start(), calls=%async_computation.9 | async-start | bytes 4325376 | tf_op jit(solution)/shard_map/reduce_scatter | solution.py:271
  513.5 4.3 copy-start.35
  513.5 214.5 %copy-start.24 = (bf16[1024,256]{1,0:T(8,128)(2,1)S(1)}, bf16[1024,256]{1,0:T(8,128)(2,1)}, u32[]{:S(2)}) copy-start(bf16[1024,256]{1,0:T(8,128)(2,1)} %param.29) | copy-start | bytes 1572868
  513.5 921.4 %reduce-scatter.10.cloned.1.call-start = ((), (), s32[]{:S(2)}) async-start(), calls=%async_computation.8 | async-start | bytes 1081344 | tf_op jit(solution)/shard_map/reduce_scatter | solution.py:270
  728.7 2.5 copy-start.15
  728.7 2.6 copy-start.21
  728.7 706.2 %copy-start.1 = (bf16[1024,1024]{1,0:T(8,128)(2,1)S(1)}, bf16[1024,1024]{1,0:T(8,128)(2,1)}, u32[]{:S(2)}) copy-start(bf16[1024,1024]{1,0:T(8,128)(2,1)} %param.34) | copy-start | bytes 6291460
  (17 other events, 22.8 us)
Sparse Core Ops, SparseCore 0:
  50.2 93.6 all-reduce.4
  157.6 92.1 all-reduce.6
  298.8 144.3 all-gather.2
  445.4 188.9 reduce-scatter.17
  639.3 223.2 reduce-scatter.15
  865.5 191.3 reduce-scatter.13
  1059.8 190.1 reduce-scatter.11
  1252.9 181.9 reduce-scatter.9
